TPU v7x, 32 devices: a 4x2x2 block of a 4x4x8 slice. The times are simulated.
32 devices in a mesh: dp: 4 (over y, z), tp: 8 (over x, core).
Axes of the slice: x: 4, y: 2, z: 2, core: 2. Of those that a mesh axis runs over, the one named last changes fastest.
The devices are a block of a 4x4x8 slice.
Arguments:
- x: bfloat16 [256, 8192], P('dp'), parts along dimension 0
- ln_attn_gamma: float32 [8192], replicated
- ln_attn_beta: float32 [8192], replicated
- ln_mlp_gamma: float32 [8192], replicated
- ln_mlp_beta: float32 [8192], replicated
- w_qkv: bfloat16 [8192, 8, 18, 64], P(None, 'tp')
- w_out: bfloat16 [8, 16, 64, 8192], P('tp')
- w_up: bfloat16 [8192, 32768], P(None, 'tp')
- w_down: bfloat16 [32768, 8192], P('tp')
- k_cache: bfloat16 [256, 8, 128, 64], P('dp', 'tp'), parts along dimension 0
- v_cache: bfloat16 [256, 8, 128, 64], P('dp', 'tp'), parts along dimension 0
- positions: int32 [256], P('dp'), parts along dimension 0
Outputs:
- output 1: bfloat16 [256, 8192], P('dp'), parts along dimension 0
- output 2: bfloat16 [256, 8, 128, 64], P('dp', 'tp'), parts along dimension 0
- output 3: bfloat16 [256, 8, 128, 64], P('dp', 'tp'), parts along dimension 0
There are 4 independent parts. A program takes and returns all parts, laid end to end along the dimension named above; an argument that names none is the same for every part.
All inputs are finite; a program needn't handle non-finite values.
Results may differ from a plain program's by a relative error of at most 0.011894.
Values are sent between devices in bfloat16 or wider.
A program may use at most 768 MiB of HBM per device.

v0:
```python
import jax
import jax.numpy as jnp
from jax import lax
from jax.sharding import PartitionSpec as P

LN_EPS = 1e-5
ROPE_BASE = 10000.0
NEG_BIG = -1e30


def layer_norm(act_rows, ln_gamma, ln_beta):
    rows_f32 = act_rows.astype(jnp.float32)
    row_mean = jnp.mean(rows_f32, axis=-1, keepdims=True)
    centred = rows_f32 - row_mean
    row_var = jnp.mean(centred * centred, axis=-1, keepdims=True)
    return (centred * lax.rsqrt(row_var + LN_EPS) * ln_gamma + ln_beta).astype(jnp.bfloat16)


def apply_rotary(vectors, cos_t, sin_t):
    half_width = vectors.shape[-1] // 2
    as_f32 = vectors.astype(jnp.float32)
    lower_half = as_f32[..., :half_width]
    upper_half = as_f32[..., half_width:]
    return jnp.concatenate([lower_half * cos_t - upper_half * sin_t, upper_half * cos_t + lower_half * sin_t], axis=-1).astype(jnp.bfloat16)


def attend_local(attn_in, w_qkv, k_cache, v_cache, positions):
    n_query = w_qkv.shape[2] - 2
    head_dim = w_qkv.shape[3]
    qkv_rows = jnp.einsum('bd,dgjh->bgjh', attn_in, w_qkv, preferred_element_type=jnp.float32).astype(jnp.bfloat16)
    inv_freq = ROPE_BASE ** (-2.0 * jnp.arange(head_dim // 2, dtype=jnp.float32) / head_dim)
    angles = positions.astype(jnp.float32)[:, None] * inv_freq[None, :]
    cos_t = jnp.cos(angles)
    sin_t = jnp.sin(angles)
    queries = apply_rotary(qkv_rows[:, :, :n_query], cos_t[:, None, None, :], sin_t[:, None, None, :])
    new_key = apply_rotary(qkv_rows[:, :, n_query], cos_t[:, None, :], sin_t[:, None, :])
    new_value = qkv_rows[:, :, n_query + 1]
    slot_ids = jnp.arange(k_cache.shape[2])
    write_mask = (slot_ids[None, :] == positions[:, None])[:, None, :, None]
    keys_all = jnp.where(write_mask, new_key[:, :, None, :], k_cache)
    values_all = jnp.where(write_mask, new_value[:, :, None, :], v_cache)
    valid_mask = (slot_ids[None, :] <= positions[:, None])[:, None, None, :]
    scores = jnp.einsum('bgqh,bgsh->bgqs', queries, keys_all, preferred_element_type=jnp.float32) * (head_dim ** -0.5)
    scores = jnp.where(valid_mask, scores, NEG_BIG)
    attn_probs = jax.nn.softmax(scores, axis=-1).astype(jnp.bfloat16)
    context = jnp.einsum('bgqs,bgsh->bgqh', attn_probs, values_all, preferred_element_type=jnp.float32).astype(jnp.bfloat16)
    return context, keys_all, values_all


def solution(mesh):
    row_spec = P('dp', None)
    vec_spec = P(None)
    cache_spec = P('dp', 'tp', None, None)

    def device_step(x, ln_attn_gamma, ln_attn_beta, ln_mlp_gamma, ln_mlp_beta, w_qkv, w_out, w_up, w_down, k_cache, v_cache, positions):
        attn_in = layer_norm(x, ln_attn_gamma, ln_attn_beta)
        mlp_in = layer_norm(x, ln_mlp_gamma, ln_mlp_beta)
        context, keys_all, values_all = attend_local(attn_in, w_qkv, k_cache, v_cache, positions)
        attn_part = jnp.einsum('bgqh,gqhd->bd', context, w_out, preferred_element_type=jnp.float32).astype(jnp.bfloat16)
        attn_total = lax.psum(attn_part, 'tp')
        hidden = jax.nn.gelu(jnp.dot(mlp_in, w_up, preferred_element_type=jnp.float32), approximate=False).astype(jnp.bfloat16)
        mlp_part = jnp.dot(hidden, w_down, preferred_element_type=jnp.float32).astype(jnp.bfloat16)
        mlp_total = lax.psum(mlp_part, 'tp')
        layer_out = (x.astype(jnp.float32) + attn_total.astype(jnp.float32) + mlp_total.astype(jnp.float32)).astype(jnp.bfloat16)
        return layer_out, keys_all, values_all

    return jax.shard_map(device_step, mesh=mesh, in_specs=(row_spec, vec_spec, vec_spec, vec_spec, vec_spec, P(None, 'tp', None, None), P('tp', None, None, None), P(None, 'tp'), P('tp', None), cache_spec, cache_spec, P('dp')), out_specs=(row_spec, cache_spec, cache_spec), check_vma=False)
```

profile of v0, /device:TPU:81, one launch (start us, length us, event | category | flops | bytes accessed | tf_op | source)
XLA Modules:
  0.0 159.5 jit_solution(16563634549284955947)
XLA Ops:
  7.2 0.0 copy-start
  7.2 0.0 copy-start.2
  7.2 0.0 copy-start.3
  7.2 0.1 all-reduce.3.cloned.1.call-start
  7.3 0.7 convert_element_type.79
  8.0 0.7 iota_compare_fusion.1
  8.8 1.5 convert_reduce_fusion
  10.2 1.7 %fusion.17 = f32[64]{0:T(128)S(1)} fusion(bf16[64,8192]{1,0:T(8,128)(2,1)} %param.12, f32[64]{0:T(128)S(1)} %broadcast_multiply_fusion), kind=kLoop, calls=%fused_computation.17 | loop fusion | flops 2097088 | bytes 1049088 | tf_op jit(solution)/shard_map/reduce_sum | solution.py:15
  11.9 0.0 copy-done
  11.9 0.0 copy-done.2
  11.9 0.0 copy-done.3
  11.9 9.1 %fusion.28 = f32[64,1152]{0,1:S(1)} fusion(bf16[8192,1152]{0,1:T(8,128)(2,1)} %bitcast.50, bf16[64,8192]{1,0:T(8,128)(2,1)S(1)} %copy-done, f32[8192]{0:T(1024)S(1)} %copy-done.2, f32[8192]{0:T(1024)S(1)} %copy-done.3, f32[64]{0:T(128)S(1)} %add_rsqrt_fusion, f32[64]{0:T(128)S(1)} %broadcast_multiply_fusion), kind=kOutput, calls=%fused_computation.29 | convolution fusion | flops 1211105280 | bytes 20283904
  21.2 0.1 multiply_cosine_fusion.1
  21.3 0.1 fusion.95
  21.5 0.1 copy.15
  21.6 0.1 copy.17
  21.7 0.1 fusion.83
  21.8 0.1 pad_maximum_fusion
  21.8 0.3 copy.16
  22.1 3.9 %broadcast_select_fusion.1 = (bf16[64,1,128,64]{2,3,1,0:T(8,128)(2,1)S(1)}, bf16[64,1,128,64]{2,3,1,0:T(8,128)(2,1)}) fusion(bf16[64,1,128,64]{2,3,1,0:T(8,128)(2,1)} %param.21, pred[64,128]{1,0:T(8,128)(4,1)S(1)} %get-tuple-element.16, bf16[64,64]{1,0:T(8,128)(2,1)S(1)} %copy.15, bf16[64,1,128,64]{2,3,1,0:T(8,128)(2,1)} %param.22, bf16[64,64]{1,0:T(8,128)(2,1)S(1)} %copy.17), kind=kLoop, calls=%fused_computation.57 | loop fusion | flops 1048576 | bytes 4218880 | tf_op jit(solution)/shard_map/jit(_where)/select_n | solution.py:40
  26.0 0.0 copy-start.1
  26.0 0.0 copy-start.4
  26.0 0.0 copy-start.5
  26.0 0.4 fusion.21
  26.4 0.3 fusion.127
  26.8 0.0 copy-done.4
  26.8 0.1 copy-done.5
  26.9 24.9 %fusion.25.clone.4 = bf16[64,4096]{1,0:T(8,128)(2,1)S(1)} fusion(bf16[8192,4096]{1,0:T(8,128)(2,1)} %param.19, bf16[64,8192]{1,0:T(8,128)(2,1)S(1)} %copy-done, f32[8192]{0:T(1024)S(1)} %copy-done.4, f32[8192]{0:T(1024)S(1)} %copy-done.5, f32[64]{0:T(128)S(1)} %add_rsqrt_fusion, f32[64]{0:T(128)S(1)} %broadcast_multiply_fusion), kind=kOutput, calls=%fused_computation.27.clone.clone.clone.1 | convolution fusion | flops 4315152384 | bytes 68747776 | tf_op jit(solution)/shard_map/dot_general | solution.py:61
  51.8 0.0 copy-done.1
  51.8 24.4 %convolution_convert_fusion = bf16[64,8192]{1,0:T(8,128)(2,1)} fusion(bf16[4096,8192]{1,0:T(8,128)(2,1)} %param.20, bf16[64,4096]{1,0:T(8,128)(2,1)S(1)} %fusion.25.clone.4), kind=kOutput, calls=%fused_computation.5 | convolution fusion | flops 4295491584 | bytes 68681728 | tf_op jit(solution)/shard_map/dot_general | solution.py:62
  76.2 3.1 %fusion.30 = bf16[64,16,64]{2,1,0:T(8,128)(2,1)S(1)} fusion(bf16[64,1,128,64]{2,3,1,0:T(8,128)(2,1)} %get-tuple-element.12, f32[64,16]{1,0:T(8,128)S(1)} %fusion.127, f32[64,16,128]{2,1,0:T(8,128)S(1)} %fusion.21), kind=kOutput, calls=%fused_computation.30 | convolution fusion | flops 17171584 | bytes 1708032 | tf_op jit(solution)/shard_map/bgqs,bgsh->bgqh/dot_general | solution.py:46
  79.3 8.5 %fusion.6 = bf16[64,8192]{1,0:T(8,128)(2,1)} fusion(bf16[1,16,64,8192]{3,2,1,0:T(8,128)(2,1)} %param.18, bf16[64,16,64]{2,1,0:T(8,128)(2,1)S(1)} %fusion.30), kind=kOutput, calls=%fused_computation.4 | convolution fusion | flops 1074266112 | bytes 17956864 | tf_op jit(solution)/shard_map/bgqh,gqhd->bd/dot_general | solution.py:59
  87.8 0.1 all-reduce.3.cloned.1.call-update
  87.9 61.8 %all-reduce.3.cloned.1.call-done = (bf16[64,8192]{1,0:T(8,128)(2,1)}, bf16[64,8192]{1,0:T(8,128)(2,1)}) async-done(((bf16[64,8192]{1,0:T(8,128)(2,1)}, bf16[64,8192]{1,0:T(8,128)(2,1)}), (bf16[64,8192]{1,0:T(8,128)(2,1)}, bf16[64,8192]{1,0:T(8,128)(2,1)})) %all-reduce.3.cloned.1.call-update) | async-done | bytes 2097168 | tf_op jit(solution)/shard_map/psum | solution.py:63
  149.7 2.9 %fusion.19 = bf16[64,8192]{1,0:T(8,128)(2,1)} fusion(bf16[64,8192]{1,0:T(8,128)(2,1)S(1)} %copy-done, bf16[64,8192]{1,0:T(8,128)(2,1)} %get-tuple-element.3, bf16[64,8192]{1,0:T(8,128)(2,1)} %get-tuple-element.4), kind=kLoop, calls=%fused_computation.19 | loop fusion | flops 3145728 | bytes 4194304 | tf_op jit(solution)/shard_map/convert_element_type | solution.py:64
  (7 shorter events, 0.1 us)
Async XLA Ops:
  7.2 4.7 %copy-start = (bf16[64,8192]{1,0:T(8,128)(2,1)S(1)}, bf16[64,8192]{1,0:T(8,128)(2,1)}, u32[]{:S(2)}) copy-start(bf16[64,8192]{1,0:T(8,128)(2,1)} %param.12) | copy-start | bytes 3145732
  7.2 4.7 %copy-start.2 = (f32[8192]{0:T(1024)S(1)}, f32[8192]{0:T(1024)}, u32[]{:S(2)}) copy-start(f32[8192]{0:T(1024)} %param.14) | copy-start | bytes 98308
  7.2 4.7 %copy-start.3 = (f32[8192]{0:T(1024)S(1)}, f32[8192]{0:T(1024)}, u32[]{:S(2)}) copy-start(f32[8192]{0:T(1024)} %param.13) | copy-start | bytes 98308
  7.2 142.5 %all-reduce.3.cloned.1.call-start = ((), (), s32[]{:S(2)}) async-start(), calls=%async_computation | async-start | bytes 4194304 | tf_op jit(solution)/shard_map/psum | solution.py:63
  26.0 25.7 %copy-start.1 = (bf16[64,1,128,64]{2,3,1,0:T(8,128)(2,1)}, bf16[64,1,128,64]{2,3,1,0:T(8,128)(2,1)S(1)}, u32[]{:S(2)}) copy-start(bf16[64,1,128,64]{2,3,1,0:T(8,128)(2,1)S(1)} %get-tuple-element.11) | copy-start | bytes 3145732
  26.0 0.8 copy-start.4
  26.0 0.8 copy-start.5
Sparse Core Ops, SparseCore 0:
  88.0 61.6 all-reduce.2
where the time goes:
time: 161 us; the launch traced here: 159 us
  matrix products  70.5 us (44%)
  waiting for transfers between devices  61.9 us (38%)
  between operations  14.2 us (9%)
  other arithmetic  12.3 us (8%)
    psum x1, waiting for transfers between devices, device_step(): mlp_total = lax.psum(mlp_part, 'tp')  61.8 us
    dot_general x1, matrix products, device_step(): jnp.dot(mlp_in, w_up, preferred_element_type=jnp.float32)  24.9 us
    dot_general x1, matrix products, device_step(): jnp.dot(hidden, w_down, preferred_element_type=jnp.float32)  24.4 us
    unnamed x1, matrix products  9.1 us
    dot_general x1, matrix products, device_step(): jnp.einsum('bgqh,gqhd->bd', context, w_out, preferred_element_type=jnp.fl...  8.54 us
    select_n x1, other arithmetic, attend_local(): keys_all = jnp.where(write_mask, new_key[:, :, None, :], k_cache)  3.94 us
  transfers between devices with their start and end apart: 1, of which 1 were waited for; matrix products, arithmetic and copies ran while one was open for 0% of the time, Pallas kernels for 0%

commit v1 on v0

v1 whole, which is shorter than its diff:
```python
import math
import numpy as np
import jax
import jax.numpy as jnp
from jax import lax
from jax.experimental import pallas as pl
from jax.experimental.pallas import tpu as pltpu
from jax.sharding import PartitionSpec as P

LN_EPS = 1e-5
ROPE_BASE = 10000.0
NEG_BIG = -1e30
F32 = jnp.float32
BF16 = jnp.bfloat16
CHUNK = 512
A_SLOTS = 4
B_SLOTS = 3


def gelu_exact(pre):
    return pre * 0.5 * (1.0 + lax.erf(pre * (1.0 / math.sqrt(2.0))))


def layer_kernel(dims, x_hbm, ga_hbm, ba_hbm, gm_hbm, bm_hbm, wqkv_hbm, wout_hbm, wup_hbm, wdown_hbm, kc_hbm, vc_hbm, pos_hbm,
                 out_hbm, ko_hbm, vo_hbm,
                 ring_a, ring_b, x_buf, attn_in, mlp_in, act, k_buf, v_buf, qkv_acc, new_kv, q_rows, ctx_rows, pre, vecs, pos_vec, pos_smem, part_buf, pair_in, sum_buf, quarter_in, out_buf,
                 sem_in, sem_qkv, sem_a, sem_b, sem_out, sem_pair, sem_quarter, sem_gather, sem_sent):
    rows, width, ff, n_query, head, seq, n_tp = dims
    qk_rows = (n_query + 2) * head
    n_qkv = width // CHUNK
    n_up = ff // CHUNK
    n_down = width // CHUNK
    ctx_w = n_query * head
    pairs = n_query // 2
    per_slot = width // qk_rows

    def qkv_row(j):
        return (j // per_slot) * width + (j % per_slot) * qk_rows

    def small_copies():
        return [
            pltpu.make_async_copy(x_hbm, x_buf, sem_in.at[0]),
            pltpu.make_async_copy(ga_hbm, vecs.at[0:1], sem_in.at[1]),
            pltpu.make_async_copy(ba_hbm, vecs.at[1:2], sem_in.at[2]),
            pltpu.make_async_copy(gm_hbm, vecs.at[2:3], sem_in.at[3]),
            pltpu.make_async_copy(bm_hbm, vecs.at[3:4], sem_in.at[4]),
            pltpu.make_async_copy(pos_hbm, pos_vec, sem_in.at[5]),
            pltpu.make_async_copy(pos_hbm, pos_smem, sem_in.at[6]),
            pltpu.make_async_copy(kc_hbm, k_buf, sem_in.at[7]),
            pltpu.make_async_copy(vc_hbm, v_buf, sem_in.at[8]),
        ]

    def qkv_copy(j):
        return pltpu.make_async_copy(wqkv_hbm.at[:, pl.ds(j * CHUNK, CHUNK)], ring_a.at[pl.ds(qkv_row(j), qk_rows), :], sem_qkv.at[j])

    def a_slot(n):
        return lax.rem(n + 3, A_SLOTS)

    def start_up(n):
        part = width // 4
        base = a_slot(n) * width
        for i in range(4):
            pltpu.make_async_copy(wup_hbm.at[pl.ds(i * part, part), pl.ds(pl.multiple_of(n * CHUNK, CHUNK), CHUNK)],
                                  ring_a.at[pl.ds(base + i * part, part), :], sem_a.at[a_slot(n)]).start()

    def wait_up(n):
        pltpu.make_async_copy(wup_hbm.at[:, pl.ds(pl.multiple_of(n * CHUNK, CHUNK), CHUNK)],
                              ring_a.at[pl.ds(a_slot(n) * width, width), :], sem_a.at[a_slot(n)]).wait()

    b_rows = ff + ctx_w

    def start_down(c):
        s = lax.rem(c, B_SLOTS)
        base = s * b_rows
        part = ff // 2
        cols = pl.ds(pl.multiple_of(c * CHUNK, CHUNK), CHUNK)
        for i in range(2):
            pltpu.make_async_copy(wdown_hbm.at[pl.ds(i * part, part), cols], ring_b.at[pl.ds(base + i * part, part), :], sem_b.at[s]).start()
        pltpu.make_async_copy(wout_hbm.at[:, cols], ring_b.at[pl.ds(base + ff, ctx_w), :], sem_b.at[s]).start()

    def wait_down(c):
        s = lax.rem(c, B_SLOTS)
        pltpu.make_async_copy(wdown_hbm.at[0:b_rows - ctx_w, pl.ds(0, CHUNK)], ring_b.at[pl.ds(s * b_rows, ff), :], sem_b.at[s]).wait()
        pltpu.make_async_copy(wout_hbm.at[:, pl.ds(0, CHUNK)], ring_b.at[pl.ds(s * b_rows + ff, ctx_w), :], sem_b.at[s]).wait()

    small = small_copies()
    for c in small:
        c.start()

    me = lax.axis_index('tp')
    n_chips = n_tp // 2
    chip, core = me // 2, lax.rem(me, 2)
    half_rows = rows // 2
    quarter = CHUNK // n_chips
    barrier = pltpu.get_barrier_semaphore()
    for d in range(1, n_tp):
        pl.semaphore_signal(barrier, inc=1, device_id={'tp': lax.rem(me + d, n_tp)}, device_id_type=pl.DeviceIdType.MESH)
    for j in range(n_qkv):
        qkv_copy(j).start()
    start_up(0)
    for c in range(B_SLOTS):
        start_down(c)

    for c in small[:5]:
        c.wait()
    lanes = 512
    n_l = width // lanes

    def fold(v):
        t = v[:, 0:128]
        for i in range(1, lanes // 128):
            t = t + v[:, i * 128:(i + 1) * 128]
        return t

    def sum_body(j, acc):
        return acc + fold(x_buf[:, pl.ds(pl.multiple_of(j * lanes, lanes), lanes)].astype(F32))

    total = lax.fori_loop(0, n_l, sum_body, jnp.zeros((rows, 128), F32))
    mean = jnp.sum(total, axis=1, keepdims=True) * (1.0 / width)

    def var_body(j, acc):
        d = x_buf[:, pl.ds(pl.multiple_of(j * lanes, lanes), lanes)].astype(F32) - mean
        return acc + fold(d * d)

    total2 = lax.fori_loop(0, n_l, var_body, jnp.zeros((rows, 128), F32))
    rstd = lax.rsqrt(jnp.sum(total2, axis=1, keepdims=True) * (1.0 / width) + LN_EPS)

    def norm_body(j, carry):
        cols = pl.ds(pl.multiple_of(j * lanes, lanes), lanes)
        nrm = (x_buf[:, cols].astype(F32) - mean) * rstd
        attn_in[0:rows, cols] = (nrm * vecs[0:1, cols] + vecs[1:2, cols]).astype(BF16)
        mlp_in[:, cols] = (nrm * vecs[2:3, cols] + vecs[3:4, cols]).astype(BF16)
        return carry

    lax.fori_loop(0, n_l, norm_body, 0)

    group = 4

    def qkv_body(g, carry):
        tot = None
        for i in range(group):
            j = g * group + i
            pltpu.make_async_copy(wqkv_hbm.at[:, pl.ds(0, CHUNK)], ring_a.at[pl.ds(0, qk_rows), :], sem_qkv.at[j]).wait()
            w = ring_a[pl.ds(pl.multiple_of(qkv_row(j), 128), qk_rows), :]
            a = attn_in[:, pl.ds(pl.multiple_of(j * CHUNK, CHUNK), CHUNK)]
            a = jnp.concatenate([a, jnp.zeros((128 - rows, CHUNK), BF16)], axis=0)
            d = lax.dot_general(w, a, (((1,), (1,)), ((), ())), preferred_element_type=F32)
            tot = d if tot is None else tot + d

        @pl.when(g == 0)
        def _():
            qkv_acc[...] = tot

        @pl.when(g > 0)
        def _():
            qkv_acc[...] += tot

        return carry

    lax.fori_loop(0, n_qkv // group, qkv_body, 0)
    for n in range(1, A_SLOTS):
        start_up(n)

    for c in small[5:]:
        c.wait()
    half = head // 2
    pos_row = jnp.concatenate([pos_vec[...], pos_vec[...]], axis=1).astype(F32)
    index = lax.broadcasted_iota(jnp.int32, (half, 128), 0).astype(F32)
    angles = jnp.exp(index * (-2.0 * math.log(ROPE_BASE) / head)) * pos_row
    cos_t = jnp.cos(angles)
    sin_t = jnp.sin(angles)

    def rotate(slot):
        u = qkv_acc[slot * head:(slot + 1) * head, :].astype(BF16).astype(F32)
        lo, hi = u[:half], u[half:]
        return jnp.concatenate([lo * cos_t - hi * sin_t, hi * cos_t + lo * sin_t], axis=0)

    for p in range(pairs):
        both = jnp.concatenate([rotate(2 * p), rotate(2 * p + 1)], axis=0)
        t = jnp.transpose(both)
        q_rows[pl.ds(p, rows, stride=pairs), :] = t[0:rows, :]
    new_kv[0:head, :] = rotate(n_query).astype(BF16)
    new_kv[head:, :] = qkv_acc[(n_query + 1) * head:, :].astype(BF16)

    scale = head ** -0.5
    lane_s = lax.broadcasted_iota(jnp.int32, (2 * head, seq), 1)
    sub_b = lax.broadcasted_iota(jnp.int32, (2 * head, seq), 0)
    lane_h = lax.broadcasted_iota(jnp.int32, (pairs, 2 * head), 1)

    def attend(b):
        pos = pos_smem[0, b]
        at_pos = lane_s == pos
        onehot = jnp.where(at_pos & (sub_b == b), 1.0, 0.0).astype(BF16)
        col = jnp.dot(new_kv[...], onehot, preferred_element_type=F32)
        r = pl.ds(pl.multiple_of(b * head, head), head)
        here = at_pos[0:head]
        keys = jnp.where(here, col[0:head], k_buf[r, :].astype(F32)).astype(BF16)
        vals = jnp.where(here, col[head:], v_buf[r, :].astype(F32)).astype(BF16)
        k_buf[r, :] = keys
        v_buf[r, :] = vals
        q2 = q_rows[pl.ds(pl.multiple_of(b * pairs, pairs), pairs), :]
        q = jnp.concatenate([jnp.where(lane_h < head, q2, 0.0), jnp.where(lane_h < head, 0.0, q2)], axis=0).astype(BF16)
        k2 = jnp.concatenate([keys, keys], axis=0)
        s = jnp.dot(q, k2, preferred_element_type=F32) * scale
        s = jnp.where(lane_s[0:2 * pairs] <= pos, s, NEG_BIG)
        e = jnp.exp(s - jnp.max(s, axis=1, keepdims=True))
        p = (e / jnp.sum(e, axis=1, keepdims=True)).astype(BF16)
        v2 = jnp.concatenate([vals, vals], axis=0)
        o = lax.dot_general(p, v2, (((1,), (1,)), ((), ())), preferred_element_type=F32)
        ctx_rows[pl.ds(pl.multiple_of(b * pairs, pairs), pairs), :] = jnp.where(lane_h < head, o[0:pairs], o[pairs:])

    batch = 8

    def attend_body(i, carry):
        for k in range(batch):
            attend(i * batch + k)
        return carry

    lax.fori_loop(0, rows // batch, attend_body, 0)
    for p in range(pairs):
        act[:, CHUNK + ff + p * 2 * head: CHUNK + ff + (p + 1) * 2 * head] = ctx_rows[pl.ds(p, rows, stride=pairs), :].astype(BF16)
    k_out = pltpu.make_async_copy(k_buf, ko_hbm, sem_out.at[0])
    v_out = pltpu.make_async_copy(v_buf, vo_hbm, sem_out.at[1])
    k_out.start()
    v_out.start()

    pre[...] = jnp.zeros_like(pre)

    def up_body(n, carry):
        @pl.when((n > 0) & (n + A_SLOTS - 1 < n_up))
        def _():
            start_up(n + A_SLOTS - 1)

        wait_up(n)
        act[:, pl.ds(pl.multiple_of(n * CHUNK, CHUNK), CHUNK)] = gelu_exact(pre[...]).astype(BF16)
        pre[...] = jnp.dot(mlp_in[...], ring_a[pl.ds(pl.multiple_of(a_slot(n) * width, width), width), :], preferred_element_type=F32)
        return carry

    lax.fori_loop(0, n_up, up_body, 0)
    act[:, ff:ff + CHUNK] = gelu_exact(pre[...]).astype(BF16)

    my_rows = pl.ds(pl.multiple_of(core * half_rows, half_rows), half_rows)
    other_rows = pl.ds(pl.multiple_of((1 - core) * half_rows, half_rows), half_rows)

    def chunk_cols(c):
        return pl.ds(pl.multiple_of(c * CHUNK, CHUNK), CHUNK)

    def quarter_cols(c, q):
        return pl.ds(pl.multiple_of(c * CHUNK + q * quarter, quarter), quarter)

    def slot_cols(c):
        return pl.ds(pl.multiple_of(c * quarter, quarter), quarter)

    def send_pair(c):
        pltpu.make_async_remote_copy(src_ref=part_buf.at[other_rows, chunk_cols(c)], dst_ref=pair_in.at[:, chunk_cols(c)],
                                     send_sem=sem_sent.at[0], recv_sem=sem_pair.at[c],
                                     device_id={'tp': chip * 2 + 1 - core}, device_id_type=pl.DeviceIdType.MESH).start()

    def send_quarters(c):
        pltpu.make_async_copy(pair_in.at[:, chunk_cols(c)], pair_in.at[:, chunk_cols(c)], sem_pair.at[c]).wait()
        both = part_buf[my_rows, chunk_cols(c)].astype(F32) + pair_in[:, chunk_cols(c)].astype(F32)
        sum_buf[:, chunk_cols(c)] = both.astype(BF16)
        for d in range(1, n_chips):
            q = lax.rem(chip + d, n_chips)
            pltpu.make_async_remote_copy(src_ref=sum_buf.at[:, quarter_cols(c, q)], dst_ref=quarter_in.at[d - 1, :, slot_cols(c)],
                                         send_sem=sem_sent.at[1], recv_sem=sem_quarter.at[d - 1, c],
                                         device_id={'tp': q * 2 + core}, device_id_type=pl.DeviceIdType.MESH).start()

    def send_result(c):
        total = x_buf[my_rows, quarter_cols(c, chip)].astype(F32) + sum_buf[:, quarter_cols(c, chip)].astype(F32)
        for d in range(1, n_chips):
            pltpu.make_async_copy(quarter_in.at[d - 1, :, slot_cols(c)], quarter_in.at[d - 1, :, slot_cols(c)], sem_quarter.at[d - 1, c]).wait()
            total = total + quarter_in[d - 1, :, slot_cols(c)].astype(F32)
        out_buf[my_rows, quarter_cols(c, chip)] = total.astype(BF16)
        for d in range(1, n_tp):
            pltpu.make_async_remote_copy(src_ref=out_buf.at[my_rows, quarter_cols(c, chip)], dst_ref=out_buf.at[my_rows, quarter_cols(c, chip)],
                                         send_sem=sem_sent.at[2], recv_sem=sem_gather.at[0],
                                         device_id={'tp': lax.rem(me + d, n_tp)}, device_id_type=pl.DeviceIdType.MESH).start()

    lag = 4
    pl.semaphore_wait(barrier, n_tp - 1)

    def down_body(c, carry):
        @pl.when((c > 0) & (c + B_SLOTS - 1 < n_down))
        def _():
            start_down(c + B_SLOTS - 1)

        wait_down(c)
        s = lax.rem(c, B_SLOTS)
        part = jnp.dot(act[:, CHUNK:], ring_b[pl.ds(pl.multiple_of(s * b_rows, 1024), b_rows), :], preferred_element_type=F32)
        part_buf[:, chunk_cols(c)] = part.astype(BF16)
        send_pair(c)

        @pl.when(c >= 1)
        def _():
            send_quarters(c - 1)

        @pl.when(c >= lag)
        def _():
            send_result(c - lag)

        return carry

    lax.fori_loop(0, n_down, down_body, 0)
    send_quarters(n_down - 1)
    for c in range(n_down - lag, n_down):
        send_result(c)

    def settle(sem, n_rows):
        pltpu.make_async_copy(out_buf.at[0:n_rows, :], out_buf.at[0:n_rows, :], sem).wait()

    settle(sem_gather.at[0], (n_tp - 1) * rows // n_tp)
    final = pltpu.make_async_copy(out_buf, out_hbm, sem_out.at[2])
    final.start()
    settle(sem_sent.at[0], rows // 2)
    settle(sem_sent.at[1], (n_chips - 1) * rows // n_tp)
    settle(sem_sent.at[2], (n_tp - 1) * rows // n_tp)
    final.wait()
    k_out.wait()
    v_out.wait()


def solution(mesh):
    row_spec = P('dp', None)
    vec_spec = P(None)
    cache_spec = P('dp', 'tp', None, None)

    def device_step(x, ga, ba, gm, bm, w_qkv, w_out, w_up, w_down, k_cache, v_cache, positions):
        rows, width = x.shape
        ff = w_up.shape[1]
        n_query, head = w_qkv.shape[2] - 2, w_qkv.shape[3]
        seq = k_cache.shape[2]
        ctx_w = n_query * head
        qk_rows = (n_query + 2) * head
        n_qkv = width // CHUNK
        n_tp = mesh.shape['tp']
        n_chips = n_tp // 2
        n_down = width // CHUNK
        dims = (rows, width, ff, n_query, head, seq, n_tp)
        wq = jnp.transpose(w_qkv, (1, 2, 3, 0)).reshape(qk_rows, width)
        wo = w_out.reshape(ctx_w, width)
        kt = jnp.transpose(k_cache, (0, 1, 3, 2)).reshape(rows * head, seq)
        vt = jnp.transpose(v_cache, (0, 1, 3, 2)).reshape(rows * head, seq)
        any_spec = pl.BlockSpec(memory_space=pl.ANY)
        out, k_new, v_new = pl.pallas_call(
            lambda *refs: layer_kernel(dims, *refs),
            name='layer',
            out_shape=(jax.ShapeDtypeStruct((rows, width), BF16), jax.ShapeDtypeStruct(kt.shape, BF16), jax.ShapeDtypeStruct(vt.shape, BF16)),
            in_specs=[any_spec] * 12,
            out_specs=(any_spec, any_spec, any_spec),
            scratch_shapes=[
                pltpu.VMEM((A_SLOTS * width, CHUNK), BF16),
                pltpu.VMEM((B_SLOTS * (ff + ctx_w), CHUNK), BF16),
                pltpu.VMEM((rows, width), BF16),
                pltpu.VMEM((rows, width), BF16),
                pltpu.VMEM((rows, width), BF16),
                pltpu.VMEM((rows, CHUNK + ff + ctx_w), BF16),
                pltpu.VMEM((rows * head, seq), BF16),
                pltpu.VMEM((rows * head, seq), BF16),
                pltpu.VMEM((qk_rows, 128), F32),
                pltpu.VMEM((2 * head, 128), BF16),
                pltpu.VMEM((rows * n_query // 2, 128), F32),
                pltpu.VMEM((rows * n_query // 2, 128), F32),
                pltpu.VMEM((rows, CHUNK), F32),
                pltpu.VMEM((4, width), F32),
                pltpu.VMEM((1, rows), jnp.int32),
                pltpu.SMEM((1, rows), jnp.int32),
                pltpu.VMEM((rows, width), BF16),
                pltpu.VMEM((rows // 2, width), BF16),
                pltpu.VMEM((rows // 2, width), BF16),
                pltpu.VMEM((n_chips - 1, rows // 2, width // n_chips), BF16),
                pltpu.VMEM((rows, width), BF16),
                pltpu.SemaphoreType.DMA((9,)),
                pltpu.SemaphoreType.DMA((n_qkv,)),
                pltpu.SemaphoreType.DMA((A_SLOTS,)),
                pltpu.SemaphoreType.DMA((B_SLOTS,)),
                pltpu.SemaphoreType.DMA((3,)),
                pltpu.SemaphoreType.DMA((n_down,)),
                pltpu.SemaphoreType.DMA((n_chips - 1, n_down)),
                pltpu.SemaphoreType.DMA((1,)),
                pltpu.SemaphoreType.DMA((3,)),
            ],
            compiler_params=pltpu.CompilerParams(vmem_limit_bytes=67043328, collective_id=0, has_side_effects=True),
        )(x, ga.reshape(1, width), ba.reshape(1, width), gm.reshape(1, width), bm.reshape(1, width), wq, wo, w_up, w_down, kt, vt, positions.reshape(1, rows))
        k_new = jnp.transpose(k_new.reshape(rows, 1, head, seq), (0, 1, 3, 2))
        v_new = jnp.transpose(v_new.reshape(rows, 1, head, seq), (0, 1, 3, 2))
        return out, k_new, v_new

    return jax.shard_map(device_step, mesh=mesh, in_specs=(row_spec, vec_spec, vec_spec, vec_spec, vec_spec, P(None, 'tp', None, None), P('tp', None, None, None), P(None, 'tp'), P('tp', None), cache_spec, cache_spec, P('dp')), out_specs=(row_spec, cache_spec, cache_spec), check_vma=False)
```

time: 161 us -> 84.6 us (0.53)
  Pallas kernels: 0 us -> 77 us
  matrix products: 70.5 us -> 0 us
  waiting for transfers between devices: 61.9 us -> 0 us
  between operations: 14.2 us -> 0.64 us
  other arithmetic: 12.3 us -> 0 us
  local copies, waits for them, and re-layouts: 0.52 us -> 6.79 us
    pallas_call x0 -> x1, Pallas kernels: none -> 77 us  [device_step(): pl.pallas_call(lambda *refs: layer_kernel(dims, *refs), name='layer', out...]
    psum x1 -> x0, waiting for transfers between devices: 61.8 us -> none  [device_step(): mlp_total = lax.psum(mlp_part, 'tp')]
    dot_general x5 -> x0, matrix products: 61.4 us -> none  [the longest x1 24.9 us: device_step(): jnp.dot(mlp_in, w_up, preferred_element_type=jnp.float32)]
    unnamed x1 -> x0, matrix products: 9.1 us -> none
    unnamed x12 -> x3, local copies, waits for them, and re-layouts: 0.08 us -> 6.79 us
    select_n x1 -> x0, other arithmetic: 3.94 us -> none  [attend_local(): keys_all = jnp.where(write_mask, new_key[:, :, None, :], k_cache)]
    convert_element_type x5 -> x0, other arithmetic: 3.71 us -> none  [the longest x1 2.88 us: device_step(): (x.astype(jnp.float32) + attn_total.astype(jnp.float32) + mlp_total.astyp...]
    reduce_sum x2 -> x0, other arithmetic: 3.13 us -> none  [the longest x1 1.67 us: layer_norm(): row_var = jnp.mean(centred * centred, axis=-1, keepdims=True)]
  transfers between devices with their start and end apart: 1 -> 0, of which waited for: 1 -> 0; matrix products, arithmetic and copies ran while one was open for 0% -> 0% of each run, Pallas kernels for 0% -> 0%
where the time goes in v1:
time: 84.6 us; the launch traced here: 84.4 us
  Pallas kernels  77 us (91%)
  local copies, waits for them, and re-layouts  6.79 us (8%)
    pallas_call x1, Pallas kernels, device_step(): pl.pallas_call(lambda *refs: layer_kernel(dims, *refs), name='layer', out...  77 us
    unnamed x3, local copies, waits for them, and re-layouts  6.79 us

profile of v1, /device:TPU:81, one launch (start us, length us, event | category | flops | bytes accessed | tf_op | source)
XLA Modules:
  0.0 84.4 jit_solution(13740904933841716182)
XLA Ops:
  0.6 77.0 %layer.1 = (bf16[64,8192]{1,0:T(8,128)(2,1)}, bf16[4096,128]{1,0:T(8,128)(2,1)}, bf16[4096,128]{1,0:T(8,128)(2,1)}) custom-call(bf16[64,8192]{1,0:T(8,128)(2,1)} %refs_0_.1, f32[1,8192]{1,0:T(1,128)} %bitcast.31, f32[1,8192]{1,0:T(1,128)} %bitcast.32, f32[1,8192]{1,0:T(1,128)} %bitcast.33, f32[1,8192]{1,0:T(1,128)} %bitcast.34, bf16[1152,8192]{1,0:T(8,128)(2,1)} %bitcast.25, ...), custom_call_target="tpu_custom_call" | custom-call | tf_op jit(solution)/shard_map/layer/pallas_call | solution.py:345
  77.6 2.3 %copy.20 = bf16[64,8192]{1,0:T(8,128)(2,1)} copy(bf16[64,8192]{1,0:T(8,128)(2,1)} %get-tuple-element.12) | data formatting | bytes 2097152
  79.9 2.3 %copy.21 = bf16[64,1,128,64]{2,3,1,0:T(8,128)(2,1)} copy(bf16[64,1,128,64]{2,3,1,0:T(8,128)(2,1)} %bitcast.30) | data formatting | bytes 2097152
  82.2 2.3 %copy.22 = bf16[64,1,128,64]{2,3,1,0:T(8,128)(2,1)} copy(bf16[64,1,128,64]{2,3,1,0:T(8,128)(2,1)} %bitcast.29) | data formatting | bytes 2097152

commit v2 on v1

v2 whole, which is shorter than its diff:
```python
import math
import numpy as np
import jax
import jax.numpy as jnp
from jax import lax
from jax.experimental import pallas as pl
from jax.experimental.pallas import tpu as pltpu
from jax.sharding import PartitionSpec as P

LN_EPS = 1e-5
ROPE_BASE = 10000.0
NEG_BIG = -1e30
F32 = jnp.float32
BF16 = jnp.bfloat16
CHUNK = 512
A_SLOTS = 4
B_SLOTS = 3
N_DIRECT = 2


def gelu_exact(pre):
    return pre * 0.5 * (1.0 + lax.erf(pre * (1.0 / math.sqrt(2.0))))


def layer_kernel(dims, x_hbm, ga_hbm, ba_hbm, gm_hbm, bm_hbm, wqkv_hbm, wout_hbm, wup_hbm, wdown_hbm, kc_hbm, vc_hbm, pos_hbm,
                 out_buf, k_buf, v_buf,
                 ring, x_buf, attn_in, mlp_in, act, qkv_acc, new_kv, q_rows, ctx_rows, pre, vecs, pos_vec, pos_smem, part_buf, pair_in, sum_buf, quarter_in, last_in,
                 sem_in, sem_qkv, sem_a, sem_b, sem_pair, sem_quarter, sem_gather, sem_last, sem_sent):
    rows, width, ff, n_query, head, seq, n_tp = dims
    qk_rows = (n_query + 2) * head
    n_qkv = width // CHUNK
    n_up = ff // CHUNK
    n_down = width // CHUNK
    ctx_w = n_query * head
    pairs = n_query // 2
    per_slot = width // qk_rows

    def qkv_row(j):
        return (j // per_slot) * width + (j % per_slot) * qk_rows

    def small_copies():
        return [
            pltpu.make_async_copy(x_hbm, x_buf, sem_in.at[0]),
            pltpu.make_async_copy(ga_hbm, vecs.at[0:1], sem_in.at[1]),
            pltpu.make_async_copy(ba_hbm, vecs.at[1:2], sem_in.at[2]),
            pltpu.make_async_copy(gm_hbm, vecs.at[2:3], sem_in.at[3]),
            pltpu.make_async_copy(bm_hbm, vecs.at[3:4], sem_in.at[4]),
            pltpu.make_async_copy(pos_hbm, pos_vec, sem_in.at[5]),
            pltpu.make_async_copy(pos_hbm, pos_smem, sem_in.at[6]),
            pltpu.make_async_copy(kc_hbm, k_buf, sem_in.at[7]),
            pltpu.make_async_copy(vc_hbm, v_buf, sem_in.at[8]),
        ]

    def qkv_copy(j):
        return pltpu.make_async_copy(wqkv_hbm.at[:, pl.ds(j * CHUNK, CHUNK)], ring.at[pl.ds(qkv_row(j), qk_rows), :], sem_qkv.at[j])

    def a_slot(n):
        return lax.rem(n + 3, A_SLOTS)

    def start_up(n):
        part = width // 4
        base = a_slot(n) * width
        for i in range(4):
            pltpu.make_async_copy(wup_hbm.at[pl.ds(i * part, part), pl.ds(pl.multiple_of(n * CHUNK, CHUNK), CHUNK)],
                                  ring.at[pl.ds(base + i * part, part), :], sem_a.at[a_slot(n)]).start()

    def wait_up(n):
        pltpu.make_async_copy(wup_hbm.at[:, pl.ds(pl.multiple_of(n * CHUNK, CHUNK), CHUNK)],
                              ring.at[pl.ds(a_slot(n) * width, width), :], sem_a.at[a_slot(n)]).wait()

    b_rows = ff + ctx_w
    n_slots = A_SLOTS + B_SLOTS
    parts = ((0, ff // 2), (ff // 2, ff // 2), (ff, ctx_w))

    def down_base(c):
        s = lax.rem(c, n_slots)
        large = lax.rem(a_slot(n_up - A_SLOTS) + s - B_SLOTS + A_SLOTS, A_SLOTS) * width
        return pl.multiple_of(jnp.where(s < B_SLOTS, A_SLOTS * width + s * b_rows, large), 1024)

    def down_copy(c, i):
        first, count = parts[i]
        cols = pl.ds(pl.multiple_of(c * CHUNK, CHUNK), CHUNK)
        src = wout_hbm.at[:, cols] if i == 2 else wdown_hbm.at[pl.ds(first, count), cols]
        return pltpu.make_async_copy(src, ring.at[pl.ds(down_base(c) + first, count), :], sem_b.at[lax.rem(c, n_slots), i])

    def start_down(c):
        for i in range(len(parts)):
            down_copy(c, i).start()

    small = small_copies()
    for c in small[:7]:
        c.start()

    me = lax.axis_index('tp')
    n_chips = n_tp // 2
    chip, core = me // 2, lax.rem(me, 2)
    half_rows = rows // 2
    quarter = CHUNK // n_chips
    barrier = pltpu.get_barrier_semaphore()
    for d in range(1, n_tp):
        pl.semaphore_signal(barrier, inc=1, device_id={'tp': lax.rem(me + d, n_tp)}, device_id_type=pl.DeviceIdType.MESH)
    for j in range(n_qkv):
        qkv_copy(j).start()

    for c in small[:5]:
        c.wait()
    lanes = 512
    n_l = width // lanes

    def fold(v):
        t = v[:, 0:128]
        for i in range(1, lanes // 128):
            t = t + v[:, i * 128:(i + 1) * 128]
        return t

    def sum_body(j, acc):
        return acc + fold(x_buf[:, pl.ds(pl.multiple_of(j * lanes, lanes), lanes)].astype(F32))

    total = lax.fori_loop(0, n_l, sum_body, jnp.zeros((rows, 128), F32))
    mean = jnp.sum(total, axis=1, keepdims=True) * (1.0 / width)

    def var_body(j, acc):
        d = x_buf[:, pl.ds(pl.multiple_of(j * lanes, lanes), lanes)].astype(F32) - mean
        return acc + fold(d * d)

    total2 = lax.fori_loop(0, n_l, var_body, jnp.zeros((rows, 128), F32))
    rstd = lax.rsqrt(jnp.sum(total2, axis=1, keepdims=True) * (1.0 / width) + LN_EPS)

    def norm_body(j, carry):
        cols = pl.ds(pl.multiple_of(j * lanes, lanes), lanes)
        nrm = (x_buf[:, cols].astype(F32) - mean) * rstd
        attn_in[0:rows, cols] = (nrm * vecs[0:1, cols] + vecs[1:2, cols]).astype(BF16)
        mlp_in[:, cols] = (nrm * vecs[2:3, cols] + vecs[3:4, cols]).astype(BF16)
        return carry

    with jax.named_scope('norm'):
        lax.fori_loop(0, n_l, norm_body, 0)

    group = 4

    def qkv_step(g):
        tot = None
        for i in range(group):
            j = g * group + i
            with jax.named_scope('qkv_wait'):
                pltpu.make_async_copy(wqkv_hbm.at[:, pl.ds(0, CHUNK)], ring.at[pl.ds(0, qk_rows), :], sem_qkv.at[j]).wait()
            w = ring[qkv_row(j):qkv_row(j) + qk_rows, :]
            a = attn_in[:, j * CHUNK:(j + 1) * CHUNK]
            d = lax.dot_general(a, w, (((1,), (1,)), ((), ())), preferred_element_type=F32)
            tot = d if tot is None else tot + d

        qkv_acc[...] = tot if g == 0 else qkv_acc[...] + tot

    for g in range(n_qkv // group):
        if g == 0:
            small[7].start()
            small[8].start()
            start_up(0)
        if g == 2:
            start_up(1)
        with jax.named_scope('qkv'):
            qkv_step(g)
    for n in range(2, A_SLOTS):
        start_up(n)
    start_down(0)

    for c in small[5:]:
        c.wait()
    half = head // 2
    pair_w = 2 * head
    pos_row = jnp.concatenate([pos_vec[...], pos_vec[...]], axis=1).astype(F32)
    pos_col = jnp.transpose(jnp.broadcast_to(pos_row, (128, 128)))[0:rows, :]
    lane = lax.broadcasted_iota(jnp.int32, (rows, pair_w), 1)
    first_half = lax.rem(lane, head) < half
    angles = jnp.exp(lax.rem(lane, half).astype(F32) * (-2.0 * math.log(ROPE_BASE) / head)) * pos_col
    cos_t = jnp.cos(angles)
    sin_t = jnp.where(first_half, -jnp.sin(angles), jnp.sin(angles))

    def rotate(u):
        swapped = jnp.where(first_half, pltpu.roll(u, pair_w - half, axis=1), pltpu.roll(u, half, axis=1))
        return u * cos_t + swapped * sin_t

    for p in range(pairs):
        q_rows[pl.ds(p, rows, stride=pairs), :] = rotate(qkv_acc[:, p * pair_w:(p + 1) * pair_w].astype(BF16).astype(F32))
    kv = qkv_acc[:, pairs * pair_w:].astype(BF16).astype(F32)
    kv = jnp.where(lane < head, rotate(kv), kv)
    new_kv[...] = jnp.transpose(jnp.concatenate([kv, jnp.zeros((128 - rows, pair_w), F32)], axis=0)).astype(BF16)

    scale = head ** -0.5
    lane_s = lax.broadcasted_iota(jnp.int32, (2 * head, seq), 1)
    sub_b = lax.broadcasted_iota(jnp.int32, (2 * head, seq), 0)
    lane_h = lax.broadcasted_iota(jnp.int32, (pairs, 2 * head), 1)

    batch = 8

    def attend_body(i, carry):
        bs = [i * batch + k for k in range(batch)]
        at = [pl.ds(pl.multiple_of(b * head, head), head) for b in bs]
        rr = [pl.ds(pl.multiple_of(b * pairs, pairs), pairs) for b in bs]
        k_old = [k_buf[r, :] for r in at]
        v_old = [v_buf[r, :] for r in at]
        q2 = [q_rows[r, :] for r in rr]
        pos = [pos_smem[0, b] for b in bs]
        pick = jnp.concatenate([jnp.where(sub_b == b, 1.0, 0.0).astype(BF16) for b in bs], axis=1)
        col = jnp.dot(new_kv[...], pick, preferred_element_type=F32)
        keys, vals, scores = [], [], []
        for k in range(batch):
            here = lane_s[0:head] == pos[k]
            c = col[:, k * seq:(k + 1) * seq]
            keys.append(jnp.where(here, c[0:head], k_old[k].astype(F32)).astype(BF16))
            vals.append(jnp.where(here, c[head:], v_old[k].astype(F32)).astype(BF16))
        for k in range(batch):
            q = jnp.concatenate([jnp.where(lane_h < head, q2[k], 0.0), jnp.where(lane_h < head, 0.0, q2[k])], axis=0).astype(BF16)
            s = jnp.dot(q, jnp.concatenate([keys[k], keys[k]], axis=0), preferred_element_type=F32) * scale
            scores.append(jnp.where(lane_s[0:2 * pairs] <= pos[k], s, NEG_BIG))
        top = [jnp.max(s, axis=1, keepdims=True) for s in scores]
        e = [jnp.exp(s - m) for s, m in zip(scores, top)]
        den = [jnp.sum(x, axis=1, keepdims=True) for x in e]
        p = [(x / d).astype(BF16) for x, d in zip(e, den)]
        o = [lax.dot_general(p[k], jnp.concatenate([vals[k], vals[k]], axis=0), (((1,), (1,)), ((), ())), preferred_element_type=F32) for k in range(batch)]
        for k in range(batch):
            ctx_rows[rr[k], :] = jnp.where(lane_h < head, o[k][0:pairs], o[k][pairs:])
        for k in range(batch):
            k_buf[at[k], :] = keys[k]
            v_buf[at[k], :] = vals[k]
        return carry

    with jax.named_scope('attend'):
        lax.fori_loop(0, rows // batch, attend_body, 0)
    for p in range(pairs):
        act[:, CHUNK + ff + p * 2 * head: CHUNK + ff + (p + 1) * 2 * head] = ctx_rows[pl.ds(p, rows, stride=pairs), :].astype(BF16)

    pre[...] = jnp.zeros_like(pre)

    def up_body(n, carry):
        @pl.when((n > 0) & (n + A_SLOTS - 1 < n_up))
        def _():
            start_up(n + A_SLOTS - 1)

        @pl.when(n + A_SLOTS - 1 == n_up)
        def _():
            for c in range(1, B_SLOTS):
                start_down(c)

        @pl.when(n + A_SLOTS - 1 >= n_up)
        def _():
            start_down(n + A_SLOTS - 1 - n_up + B_SLOTS)

        with jax.named_scope('up_wait'):
            wait_up(n)
        act[:, pl.ds(pl.multiple_of(n * CHUNK, CHUNK), CHUNK)] = gelu_exact(pre[...]).astype(BF16)
        pre[...] = jnp.dot(mlp_in[...], ring[pl.ds(pl.multiple_of(a_slot(n) * width, width), width), :], preferred_element_type=F32)
        return carry

    with jax.named_scope('up'):
        lax.fori_loop(0, n_up, up_body, 0)
    act[:, ff:ff + CHUNK] = gelu_exact(pre[...]).astype(BF16)

    n_paired = n_down - N_DIRECT
    my_rows = pl.ds(pl.multiple_of(core * half_rows, half_rows), half_rows)
    other_rows = pl.ds(pl.multiple_of((1 - core) * half_rows, half_rows), half_rows)

    def chunk_cols(c):
        return pl.ds(pl.multiple_of(c * CHUNK, CHUNK), CHUNK)

    def quarter_cols(c, q):
        return pl.ds(pl.multiple_of(c * CHUNK + q * quarter, quarter), quarter)

    def slot_cols(c):
        return pl.ds(pl.multiple_of(c * quarter, quarter), quarter)

    def send_pair(c):
        pltpu.make_async_remote_copy(src_ref=part_buf.at[other_rows, chunk_cols(c)], dst_ref=pair_in.at[:, chunk_cols(c)],
                                     send_sem=sem_sent.at[0], recv_sem=sem_pair.at[c],
                                     device_id={'tp': chip * 2 + 1 - core}, device_id_type=pl.DeviceIdType.MESH).start()

    def send_quarters(c):
        pltpu.make_async_copy(pair_in.at[:, chunk_cols(c)], pair_in.at[:, chunk_cols(c)], sem_pair.at[c]).wait()
        both = part_buf[my_rows, chunk_cols(c)].astype(F32) + pair_in[:, chunk_cols(c)].astype(F32)
        sum_buf[:, chunk_cols(c)] = both.astype(BF16)
        for d in sorted(range(1, n_chips), key=lambda d: -min(d, n_chips - d)):
            q = lax.rem(chip + d, n_chips)
            pltpu.make_async_remote_copy(src_ref=sum_buf.at[:, quarter_cols(c, q)], dst_ref=quarter_in.at[d - 1, :, slot_cols(c)],
                                         send_sem=sem_sent.at[1], recv_sem=sem_quarter.at[d - 1, c],
                                         device_id={'tp': q * 2 + core}, device_id_type=pl.DeviceIdType.MESH).start()

    def send_result(c):
        total = x_buf[my_rows, quarter_cols(c, chip)].astype(F32) + sum_buf[:, quarter_cols(c, chip)].astype(F32)
        for d in range(1, n_chips):
            pltpu.make_async_copy(quarter_in.at[d - 1, :, slot_cols(c)], quarter_in.at[d - 1, :, slot_cols(c)], sem_quarter.at[d - 1, c]).wait()
            total = total + quarter_in[d - 1, :, slot_cols(c)].astype(F32)
        gather(c, total)

    def gather(c, total):
        out_buf[my_rows, quarter_cols(c, chip)] = total.astype(BF16)
        for d in sorted(range(1, n_tp), key=lambda d: -min(d, n_tp - d)):
            pltpu.make_async_remote_copy(src_ref=out_buf.at[my_rows, quarter_cols(c, chip)], dst_ref=out_buf.at[my_rows, quarter_cols(c, chip)],
                                         send_sem=sem_sent.at[2], recv_sem=sem_gather.at[0],
                                         device_id={'tp': lax.rem(me + d, n_tp)}, device_id_type=pl.DeviceIdType.MESH).start()

    def send_direct(c):
        for d in sorted(range(1, n_tp), key=lambda d: -min(d, n_tp - d)):
            to = lax.rem(me + d, n_tp)
            src = part_buf.at[pl.ds(pl.multiple_of(lax.rem(to, 2) * half_rows, half_rows), half_rows), quarter_cols(c, to // 2)]
            pltpu.make_async_remote_copy(src_ref=src, dst_ref=last_in.at[c - n_paired, d - 1], send_sem=sem_sent.at[3], recv_sem=sem_last.at[c - n_paired, d - 1],
                                         device_id={'tp': to}, device_id_type=pl.DeviceIdType.MESH).start()

    def send_result_direct(c):
        total = x_buf[my_rows, quarter_cols(c, chip)].astype(F32) + part_buf[my_rows, quarter_cols(c, chip)].astype(F32)
        for d in range(1, n_tp):
            pltpu.make_async_copy(last_in.at[c - n_paired, d - 1], last_in.at[c - n_paired, d - 1], sem_last.at[c - n_paired, d - 1]).wait()
            total = total + last_in[c - n_paired, d - 1].astype(F32)
        gather(c, total)

    lag = 4
    pl.semaphore_wait(barrier, n_tp - 1)
    start_down(n_slots - 1)

    def multiply(c, groups):
        total = None
        for group in groups:
            with jax.named_scope('down_wait'):
                for i in group:
                    down_copy(c, i).wait()
            first, count = parts[group[0]][0], sum(parts[i][1] for i in group)
            w = ring[pl.ds(down_base(c) + first, count), :]
            d = jnp.dot(act[:, CHUNK + first:CHUNK + first + count], w, preferred_element_type=F32)
            total = d if total is None else total + d
        part_buf[:, chunk_cols(c)] = total.astype(BF16)

    def down_body(c, carry):
        @pl.when((c > 0) & (c + n_slots - 1 < n_down))
        def _():
            start_down(c + n_slots - 1)

        multiply(c, ((0, 1, 2),))
        send_pair(c)

        @pl.when(c >= 1)
        def _():
            with jax.named_scope('quarters'):
                send_quarters(c - 1)

        @pl.when(c >= lag)
        def _():
            with jax.named_scope('result'):
                send_result(c - lag)

        return carry

    with jax.named_scope('down'):
        lax.fori_loop(0, n_paired, down_body, 0)
    done = n_paired - lag
    for c in range(n_paired, n_down):
        with jax.named_scope('tail_multiply'):
            multiply(c, ((0, 1, 2),) if c < n_down - 1 else ((0,), (1,), (2,)))
        send_direct(c)
        if c == n_paired:
            with jax.named_scope('tail_quarters'):
                send_quarters(c - 1)
        with jax.named_scope('tail_result'):
            send_result(done)
        done += 1
    for c in range(done, n_paired):
        with jax.named_scope('tail_result'):
            send_result(c)
    for c in range(n_paired, n_down):
        with jax.named_scope('tail_direct'):
            send_result_direct(c)

    def settle(sem, n_rows):
        pltpu.make_async_copy(out_buf.at[0:n_rows, :], out_buf.at[0:n_rows, :], sem).wait()

    with jax.named_scope('gather_wait'):
        settle(sem_gather.at[0], (n_tp - 1) * rows // n_tp)
    with jax.named_scope('sent_wait'):
        sent = pltpu.make_async_copy(part_buf.at[other_rows, 0:n_paired * CHUNK], part_buf.at[other_rows, 0:n_paired * CHUNK], sem_sent.at[0])
        sent.wait()
        for d in range(1, n_chips):
            pltpu.make_async_copy(quarter_in.at[d - 1, :, 0:n_paired * quarter], quarter_in.at[d - 1, :, 0:n_paired * quarter], sem_sent.at[1]).wait()
        settle(sem_sent.at[2], (n_tp - 1) * rows // n_tp)
        pltpu.make_async_copy(last_in, last_in, sem_sent.at[3]).wait()


def write_kernel(a_ref, b_ref, c_ref, a_out, b_out, c_out, sem):
    copies = []
    for i, (src, dst) in enumerate(((a_ref, a_out), (b_ref, b_out), (c_ref, c_out))):
        copies.append(pltpu.make_async_copy(src, dst, sem.at[i]))
    for c in copies:
        c.start()
    for c in copies:
        c.wait()


def solution(mesh):
    row_spec = P('dp', None)
    vec_spec = P(None)
    cache_spec = P('dp', 'tp', None, None)

    def device_step(x, ga, ba, gm, bm, w_qkv, w_out, w_up, w_down, k_cache, v_cache, positions):
        rows, width = x.shape
        ff = w_up.shape[1]
        n_query, head = w_qkv.shape[2] - 2, w_qkv.shape[3]
        seq = k_cache.shape[2]
        ctx_w = n_query * head
        qk_rows = (n_query + 2) * head
        n_qkv = width // CHUNK
        n_tp = mesh.shape['tp']
        n_chips = n_tp // 2
        n_down = width // CHUNK
        dims = (rows, width, ff, n_query, head, seq, n_tp)
        wq = jnp.transpose(w_qkv, (1, 2, 3, 0)).reshape(qk_rows, width)
        wo = w_out.reshape(ctx_w, width)
        kt = jnp.transpose(k_cache, (0, 1, 3, 2)).reshape(rows * head, seq)
        vt = jnp.transpose(v_cache, (0, 1, 3, 2)).reshape(rows * head, seq)
        any_spec = pl.BlockSpec(memory_space=pl.ANY)
        vmem_spec = pl.BlockSpec(memory_space=pltpu.VMEM)
        out, k_new, v_new = pl.pallas_call(
            lambda *refs: layer_kernel(dims, *refs),
            name='layer',
            out_shape=(pltpu.VMEM((rows, width), BF16), pltpu.VMEM(kt.shape, BF16), pltpu.VMEM(vt.shape, BF16)),
            in_specs=[any_spec] * 12,
            out_specs=(vmem_spec, vmem_spec, vmem_spec),
            scratch_shapes=[
                pltpu.VMEM((A_SLOTS * width + B_SLOTS * (ff + ctx_w), CHUNK), BF16),
                pltpu.VMEM((rows, width), BF16),
                pltpu.VMEM((rows, width), BF16),
                pltpu.VMEM((rows, width), BF16),
                pltpu.VMEM((rows, CHUNK + ff + ctx_w), BF16),
                pltpu.VMEM((rows, qk_rows), F32),
                pltpu.VMEM((2 * head, 128), BF16),
                pltpu.VMEM((rows * n_query // 2, 128), F32),
                pltpu.VMEM((rows * n_query // 2, 128), F32),
                pltpu.VMEM((rows, CHUNK), F32),
                pltpu.VMEM((4, width), F32),
                pltpu.VMEM((1, rows), jnp.int32),
                pltpu.SMEM((1, rows), jnp.int32),
                pltpu.VMEM((rows, width), BF16),
                pltpu.VMEM((rows // 2, width), BF16),
                pltpu.VMEM((rows // 2, width), BF16),
                pltpu.VMEM((n_chips - 1, rows // 2, width // n_chips), BF16),
                pltpu.VMEM((N_DIRECT, n_tp - 1, rows // 2, CHUNK // n_chips), BF16),
                pltpu.SemaphoreType.DMA((9,)),
                pltpu.SemaphoreType.DMA((n_qkv,)),
                pltpu.SemaphoreType.DMA((A_SLOTS,)),
                pltpu.SemaphoreType.DMA((A_SLOTS + B_SLOTS, 3)),
                pltpu.SemaphoreType.DMA((n_down,)),
                pltpu.SemaphoreType.DMA((n_chips - 1, n_down)),
                pltpu.SemaphoreType.DMA((1,)),
                pltpu.SemaphoreType.DMA((N_DIRECT, n_tp - 1)),
                pltpu.SemaphoreType.DMA((4,)),
            ],
            compiler_params=pltpu.CompilerParams(vmem_limit_bytes=60 * 1024 * 1024, collective_id=0, has_side_effects=True),
        )(x, ga.reshape(1, width), ba.reshape(1, width), gm.reshape(1, width), bm.reshape(1, width), wq, wo, w_up, w_down, kt, vt, positions.reshape(1, rows))
        out, k_new, v_new = (pltpu.with_memory_space_constraint(v, pltpu.VMEM) for v in (out, k_new, v_new))
        out, k_new, v_new = pl.pallas_call(
            write_kernel,
            name='write',
            out_shape=(jax.ShapeDtypeStruct((rows, width), BF16), jax.ShapeDtypeStruct(kt.shape, BF16), jax.ShapeDtypeStruct(vt.shape, BF16)),
            in_specs=[vmem_spec] * 3,
            out_specs=(any_spec, any_spec, any_spec),
            scratch_shapes=[pltpu.SemaphoreType.DMA((3,))],
            compiler_params=pltpu.CompilerParams(vmem_limit_bytes=1024 * 1024),
        )(out, k_new, v_new)
        k_new = jnp.transpose(k_new.reshape(rows, 1, head, seq), (0, 1, 3, 2))
        v_new = jnp.transpose(v_new.reshape(rows, 1, head, seq), (0, 1, 3, 2))
        return out, k_new, v_new

    return jax.shard_map(device_step, mesh=mesh, in_specs=(row_spec, vec_spec, vec_spec, vec_spec, vec_spec, P(None, 'tp', None, None), P('tp', None, None, None), P(None, 'tp'), P('tp', None), cache_spec, cache_spec, P('dp')), out_specs=(row_spec, cache_spec, cache_spec), check_vma=False)
```

time: 84.6 us -> 65.9 us (0.78)
  Pallas kernels: 77 us -> 65.2 us
  local copies, waits for them, and re-layouts: 6.79 us -> 0 us
    pallas_call x1, Pallas kernels: 77 us -> 63.5 us  [device_step(): pl.pallas_call(lambda *refs: layer_kernel(dims, *refs), name='layer', out...]
    unnamed x3 -> x0, local copies, waits for them, and re-layouts: 6.79 us -> none
    pallas_call x0 -> x1, Pallas kernels: none -> 1.69 us  [device_step(): pl.pallas_call(write_kernel, name='write', out_shape=(jax.ShapeDtypeStruc...]
where the time goes in v2:
time: 65.9 us; the launch traced here: 65.8 us
  Pallas kernels  65.2 us (99%)
    pallas_call x1, Pallas kernels, device_step(): pl.pallas_call(lambda *refs: layer_kernel(dims, *refs), name='layer', out...  63.5 us
    pallas_call x1, Pallas kernels, device_step(): pl.pallas_call(write_kernel, name='write', out_shape=(jax.ShapeDtypeStruc...  1.69 us

profile of v2, /device:TPU:81, one launch (start us, length us, event | category | flops | bytes accessed | tf_op | source)
XLA Modules:
  0.0 65.8 jit_solution(6856508098532787957)
XLA Ops:
  0.6 63.5 %layer.1 = (bf16[64,8192]{1,0:T(8,128)(2,1)S(1)}, bf16[4096,128]{1,0:T(8,128)(2,1)S(1)}, bf16[4096,128]{1,0:T(8,128)(2,1)S(1)}) custom-call(bf16[64,8192]{1,0:T(8,128)(2,1)} %refs_0_.1, f32[1,8192]{1,0:T(1,128)} %bitcast.29, f32[1,8192]{1,0:T(1,128)} %bitcast.30, f32[1,8192]{1,0:T(1,128)} %bitcast.31, f32[1,8192]{1,0:T(1,128)} %bitcast.32, ...), custom_call_target="tpu_custom_call" | custom-call | tf_op jit(solution)/shard_map/layer/pallas_call | solution.py:418
  64.1 1.7 %write.1 = (bf16[64,8192]{1,0:T(8,128)(2,1)}, bf16[4096,128]{1,0:T(8,128)(2,1)}, bf16[4096,128]{1,0:T(8,128)(2,1)}) custom-call(bf16[64,8192]{1,0:T(8,128)(2,1)S(1)} %get-tuple-element.9.a_ref, bf16[4096,128]{1,0:T(8,128)(2,1)S(1)} %get-tuple-element.10.b_ref, bf16[4096,128]{1,0:T(8,128)(2,1)S(1)} %get-tuple-element.11.c_ref), custom_call_target="tpu_custom_call" | custom-call | tf_op jit(solution)/shard_map/write/pallas_call | solution.py:456

commit v3 on v2

--- a/solution.py
+++ b/solution.py
@@ -16,6 +16,7 @@
 A_SLOTS = 4
 B_SLOTS = 3
 N_DIRECT = 2
+QKV_GROUP = 4
 
 
 def gelu_exact(pre):
@@ -34,6 +35,7 @@
     ctx_w = n_query * head
     pairs = n_query // 2
     per_slot = width // qk_rows
+    group = QKV_GROUP
 
     def qkv_row(j):
         return (j // per_slot) * width + (j % per_slot) * qk_rows
@@ -42,17 +44,17 @@
         return [
             pltpu.make_async_copy(x_hbm, x_buf, sem_in.at[0]),
             pltpu.make_async_copy(ga_hbm, vecs.at[0:1], sem_in.at[1]),
-            pltpu.make_async_copy(ba_hbm, vecs.at[1:2], sem_in.at[2]),
-            pltpu.make_async_copy(gm_hbm, vecs.at[2:3], sem_in.at[3]),
-            pltpu.make_async_copy(bm_hbm, vecs.at[3:4], sem_in.at[4]),
-            pltpu.make_async_copy(pos_hbm, pos_vec, sem_in.at[5]),
-            pltpu.make_async_copy(pos_hbm, pos_smem, sem_in.at[6]),
-            pltpu.make_async_copy(kc_hbm, k_buf, sem_in.at[7]),
-            pltpu.make_async_copy(vc_hbm, v_buf, sem_in.at[8]),
+            pltpu.make_async_copy(ba_hbm, vecs.at[1:2], sem_in.at[1]),
+            pltpu.make_async_copy(gm_hbm, vecs.at[2:3], sem_in.at[1]),
+            pltpu.make_async_copy(bm_hbm, vecs.at[3:4], sem_in.at[1]),
+            pltpu.make_async_copy(pos_hbm, pos_vec, sem_in.at[2]),
+            pltpu.make_async_copy(pos_hbm, pos_smem, sem_in.at[3]),
+            pltpu.make_async_copy(kc_hbm, k_buf, sem_in.at[4]),
+            pltpu.make_async_copy(vc_hbm, v_buf, sem_in.at[4]),
         ]
 
     def qkv_copy(j):
-        return pltpu.make_async_copy(wqkv_hbm.at[:, pl.ds(j * CHUNK, CHUNK)], ring.at[pl.ds(qkv_row(j), qk_rows), :], sem_qkv.at[j])
+        return pltpu.make_async_copy(wqkv_hbm.at[:, pl.ds(j * CHUNK, CHUNK)], ring.at[pl.ds(qkv_row(j), qk_rows), :], sem_qkv.at[j // group])
 
     def a_slot(n):
         return lax.rem(n + 3, A_SLOTS)
@@ -77,15 +79,19 @@
         large = lax.rem(a_slot(n_up - A_SLOTS) + s - B_SLOTS + A_SLOTS, A_SLOTS) * width
         return pl.multiple_of(jnp.where(s < B_SLOTS, A_SLOTS * width + s * b_rows, large), 1024)
 
-    def down_copy(c, i):
+    def down_copy(c, i, sem):
         first, count = parts[i]
         cols = pl.ds(pl.multiple_of(c * CHUNK, CHUNK), CHUNK)
         src = wout_hbm.at[:, cols] if i == 2 else wdown_hbm.at[pl.ds(first, count), cols]
-        return pltpu.make_async_copy(src, ring.at[pl.ds(down_base(c) + first, count), :], sem_b.at[lax.rem(c, n_slots), i])
+        return pltpu.make_async_copy(src, ring.at[pl.ds(down_base(c) + first, count), :], sem)
 
     def start_down(c):
         for i in range(len(parts)):
-            down_copy(c, i).start()
+            down_copy(c, i, sem_b.at[lax.rem(c, n_slots)]).start()
+
+    def start_last_down():
+        for i in range(len(parts)):
+            down_copy(n_down - 1, i, sem_b.at[n_slots + i]).start()
 
     small = small_copies()
     for c in small[:7]:
@@ -136,14 +142,14 @@
     with jax.named_scope('norm'):
         lax.fori_loop(0, n_l, norm_body, 0)
 
-    group = 4
 
     def qkv_step(g):
         tot = None
+        with jax.named_scope('qkv_wait'):
+            for i in range(group):
+                qkv_copy(g * group + i).wait()
         for i in range(group):
             j = g * group + i
-            with jax.named_scope('qkv_wait'):
-                pltpu.make_async_copy(wqkv_hbm.at[:, pl.ds(0, CHUNK)], ring.at[pl.ds(0, qk_rows), :], sem_qkv.at[j]).wait()
             w = ring[qkv_row(j):qkv_row(j) + qk_rows, :]
             a = attn_in[:, j * CHUNK:(j + 1) * CHUNK]
             d = lax.dot_general(a, w, (((1,), (1,)), ((), ())), preferred_element_type=F32)
@@ -281,13 +287,13 @@
         for d in sorted(range(1, n_chips), key=lambda d: -min(d, n_chips - d)):
             q = lax.rem(chip + d, n_chips)
             pltpu.make_async_remote_copy(src_ref=sum_buf.at[:, quarter_cols(c, q)], dst_ref=quarter_in.at[d - 1, :, slot_cols(c)],
-                                         send_sem=sem_sent.at[1], recv_sem=sem_quarter.at[d - 1, c],
+                                         send_sem=sem_sent.at[1], recv_sem=sem_quarter.at[c],
                                          device_id={'tp': q * 2 + core}, device_id_type=pl.DeviceIdType.MESH).start()
 
     def send_result(c):
         total = x_buf[my_rows, quarter_cols(c, chip)].astype(F32) + sum_buf[:, quarter_cols(c, chip)].astype(F32)
+        pltpu.make_async_copy(quarter_in.at[:, :, slot_cols(c)], quarter_in.at[:, :, slot_cols(c)], sem_quarter.at[c]).wait()
         for d in range(1, n_chips):
-            pltpu.make_async_copy(quarter_in.at[d - 1, :, slot_cols(c)], quarter_in.at[d - 1, :, slot_cols(c)], sem_quarter.at[d - 1, c]).wait()
             total = total + quarter_in[d - 1, :, slot_cols(c)].astype(F32)
         gather(c, total)
 
@@ -302,13 +308,13 @@
         for d in sorted(range(1, n_tp), key=lambda d: -min(d, n_tp - d)):
             to = lax.rem(me + d, n_tp)
             src = part_buf.at[pl.ds(pl.multiple_of(lax.rem(to, 2) * half_rows, half_rows), half_rows), quarter_cols(c, to // 2)]
-            pltpu.make_async_remote_copy(src_ref=src, dst_ref=last_in.at[c - n_paired, d - 1], send_sem=sem_sent.at[3], recv_sem=sem_last.at[c - n_paired, d - 1],
+            pltpu.make_async_remote_copy(src_ref=src, dst_ref=last_in.at[c - n_paired, d - 1], send_sem=sem_sent.at[3], recv_sem=sem_last.at[c - n_paired],
                                          device_id={'tp': to}, device_id_type=pl.DeviceIdType.MESH).start()
 
     def send_result_direct(c):
         total = x_buf[my_rows, quarter_cols(c, chip)].astype(F32) + part_buf[my_rows, quarter_cols(c, chip)].astype(F32)
+        pltpu.make_async_copy(last_in.at[c - n_paired], last_in.at[c - n_paired], sem_last.at[c - n_paired]).wait()
         for d in range(1, n_tp):
-            pltpu.make_async_copy(last_in.at[c - n_paired, d - 1], last_in.at[c - n_paired, d - 1], sem_last.at[c - n_paired, d - 1]).wait()
             total = total + last_in[c - n_paired, d - 1].astype(F32)
         gather(c, total)
 
@@ -318,20 +324,24 @@
 
     def multiply(c, groups):
         total = None
-        for group in groups:
+        for span in groups:
             with jax.named_scope('down_wait'):
-                for i in group:
-                    down_copy(c, i).wait()
-            first, count = parts[group[0]][0], sum(parts[i][1] for i in group)
+                for i in span:
+                    down_copy(c, i, sem_b.at[n_slots + i] if len(groups) > 1 else sem_b.at[lax.rem(c, n_slots)]).wait()
+            first, count = parts[span[0]][0], sum(parts[i][1] for i in span)
             w = ring[pl.ds(down_base(c) + first, count), :]
             d = jnp.dot(act[:, CHUNK + first:CHUNK + first + count], w, preferred_element_type=F32)
             total = d if total is None else total + d
         part_buf[:, chunk_cols(c)] = total.astype(BF16)
 
     def down_body(c, carry):
-        @pl.when((c > 0) & (c + n_slots - 1 < n_down))
+        @pl.when((c > 0) & (c + n_slots < n_down))
         def _():
             start_down(c + n_slots - 1)
+
+        @pl.when(c + n_slots == n_down)
+        def _():
+            start_last_down()
 
         multiply(c, ((0, 1, 2),))
         send_pair(c)
@@ -440,14 +450,14 @@
                 pltpu.VMEM((rows // 2, width), BF16),
                 pltpu.VMEM((n_chips - 1, rows // 2, width // n_chips), BF16),
                 pltpu.VMEM((N_DIRECT, n_tp - 1, rows // 2, CHUNK // n_chips), BF16),
-                pltpu.SemaphoreType.DMA((9,)),
-                pltpu.SemaphoreType.DMA((n_qkv,)),
+                pltpu.SemaphoreType.DMA((5,)),
+                pltpu.SemaphoreType.DMA((n_qkv // QKV_GROUP,)),
                 pltpu.SemaphoreType.DMA((A_SLOTS,)),
-                pltpu.SemaphoreType.DMA((A_SLOTS + B_SLOTS, 3)),
-                pltpu.SemaphoreType.DMA((n_down,)),
-                pltpu.SemaphoreType.DMA((n_chips - 1, n_down)),
+                pltpu.SemaphoreType.DMA((A_SLOTS + B_SLOTS + 3,)),
+                pltpu.SemaphoreType.DMA((n_down - N_DIRECT,)),
+                pltpu.SemaphoreType.DMA((n_down - N_DIRECT,)),
                 pltpu.SemaphoreType.DMA((1,)),
-                pltpu.SemaphoreType.DMA((N_DIRECT, n_tp - 1)),
+                pltpu.SemaphoreType.DMA((N_DIRECT,)),
                 pltpu.SemaphoreType.DMA((4,)),
             ],
             compiler_params=pltpu.CompilerParams(vmem_limit_bytes=60 * 1024 * 1024, collective_id=0, has_side_effects=True),

time: 65.9 us -> 65.2 us (0.989)
  Pallas kernels: 65.2 us -> 64.5 us
    pallas_call x1, Pallas kernels: 63.5 us -> 62.8 us  [device_step(): pl.pallas_call(lambda *refs: layer_kernel(dims, *refs), name='layer', out...]
where the time goes in v3:
time: 65.2 us
  Pallas kernels  64.5 us (99%)
    pallas_call x1, Pallas kernels, device_step(): pl.pallas_call(lambda *refs: layer_kernel(dims, *refs), name='layer', out...  62.8 us
    pallas_call x1, Pallas kernels, device_step(): pl.pallas_call(write_kernel, name='write', out_shape=(jax.ShapeDtypeStruc...  1.69 us

profile of v3, /device:TPU:81, one launch (start us, length us, event | category | flops | bytes accessed | tf_op | source)
XLA Modules:
  0.0 65.2 jit_solution(1536764636526441078)
XLA Ops:
  0.6 62.8 %layer.1 = (bf16[64,8192]{1,0:T(8,128)(2,1)S(1)}, bf16[4096,128]{1,0:T(8,128)(2,1)S(1)}, bf16[4096,128]{1,0:T(8,128)(2,1)S(1)}) custom-call(bf16[64,8192]{1,0:T(8,128)(2,1)} %refs_0_.1, f32[1,8192]{1,0:T(1,128)} %bitcast.29, f32[1,8192]{1,0:T(1,128)} %bitcast.30, f32[1,8192]{1,0:T(1,128)} %bitcast.31, f32[1,8192]{1,0:T(1,128)} %bitcast.32, ...), custom_call_target="tpu_custom_call" | custom-call | tf_op jit(solution)/shard_map/layer/pallas_call | solution.py:428
  63.5 1.7 %write.1 = (bf16[64,8192]{1,0:T(8,128)(2,1)}, bf16[4096,128]{1,0:T(8,128)(2,1)}, bf16[4096,128]{1,0:T(8,128)(2,1)}) custom-call(bf16[64,8192]{1,0:T(8,128)(2,1)S(1)} %get-tuple-element.9.a_ref, bf16[4096,128]{1,0:T(8,128)(2,1)S(1)} %get-tuple-element.10.b_ref, bf16[4096,128]{1,0:T(8,128)(2,1)S(1)} %get-tuple-element.11.c_ref), custom_call_target="tpu_custom_call" | custom-call | tf_op jit(solution)/shard_map/write/pallas_call | solution.py:466

commit v4 on v3

--- a/solution.py
+++ b/solution.py
@@ -16,6 +16,8 @@
 A_SLOTS = 4
 B_SLOTS = 3
 N_DIRECT = 2
+PAIR_SEMS = 4
+QUARTER_SEMS = 8
 QKV_GROUP = 4
 
 
@@ -43,14 +45,14 @@
     def small_copies():
         return [
             pltpu.make_async_copy(x_hbm, x_buf, sem_in.at[0]),
-            pltpu.make_async_copy(ga_hbm, vecs.at[0:1], sem_in.at[1]),
-            pltpu.make_async_copy(ba_hbm, vecs.at[1:2], sem_in.at[1]),
-            pltpu.make_async_copy(gm_hbm, vecs.at[2:3], sem_in.at[1]),
-            pltpu.make_async_copy(bm_hbm, vecs.at[3:4], sem_in.at[1]),
-            pltpu.make_async_copy(pos_hbm, pos_vec, sem_in.at[2]),
-            pltpu.make_async_copy(pos_hbm, pos_smem, sem_in.at[3]),
-            pltpu.make_async_copy(kc_hbm, k_buf, sem_in.at[4]),
-            pltpu.make_async_copy(vc_hbm, v_buf, sem_in.at[4]),
+            pltpu.make_async_copy(ga_hbm, vecs.at[0:1], sem_in.at[0]),
+            pltpu.make_async_copy(ba_hbm, vecs.at[1:2], sem_in.at[0]),
+            pltpu.make_async_copy(gm_hbm, vecs.at[2:3], sem_in.at[0]),
+            pltpu.make_async_copy(bm_hbm, vecs.at[3:4], sem_in.at[0]),
+            pltpu.make_async_copy(pos_hbm, pos_vec, sem_in.at[1]),
+            pltpu.make_async_copy(pos_hbm, pos_smem, sem_in.at[1]),
+            pltpu.make_async_copy(kc_hbm, k_buf, sem_in.at[1]),
+            pltpu.make_async_copy(vc_hbm, v_buf, sem_in.at[1]),
         ]
 
     def qkv_copy(j):
@@ -277,22 +279,22 @@
 
     def send_pair(c):
         pltpu.make_async_remote_copy(src_ref=part_buf.at[other_rows, chunk_cols(c)], dst_ref=pair_in.at[:, chunk_cols(c)],
-                                     send_sem=sem_sent.at[0], recv_sem=sem_pair.at[c],
+                                     send_sem=sem_sent.at[0], recv_sem=sem_pair.at[lax.rem(c, PAIR_SEMS)],
                                      device_id={'tp': chip * 2 + 1 - core}, device_id_type=pl.DeviceIdType.MESH).start()
 
     def send_quarters(c):
-        pltpu.make_async_copy(pair_in.at[:, chunk_cols(c)], pair_in.at[:, chunk_cols(c)], sem_pair.at[c]).wait()
+        pltpu.make_async_copy(pair_in.at[:, chunk_cols(c)], pair_in.at[:, chunk_cols(c)], sem_pair.at[lax.rem(c, PAIR_SEMS)]).wait()
         both = part_buf[my_rows, chunk_cols(c)].astype(F32) + pair_in[:, chunk_cols(c)].astype(F32)
         sum_buf[:, chunk_cols(c)] = both.astype(BF16)
         for d in sorted(range(1, n_chips), key=lambda d: -min(d, n_chips - d)):
             q = lax.rem(chip + d, n_chips)
             pltpu.make_async_remote_copy(src_ref=sum_buf.at[:, quarter_cols(c, q)], dst_ref=quarter_in.at[d - 1, :, slot_cols(c)],
-                                         send_sem=sem_sent.at[1], recv_sem=sem_quarter.at[c],
+                                         send_sem=sem_sent.at[0], recv_sem=sem_quarter.at[lax.rem(c, QUARTER_SEMS)],
                                          device_id={'tp': q * 2 + core}, device_id_type=pl.DeviceIdType.MESH).start()
 
     def send_result(c):
         total = x_buf[my_rows, quarter_cols(c, chip)].astype(F32) + sum_buf[:, quarter_cols(c, chip)].astype(F32)
-        pltpu.make_async_copy(quarter_in.at[:, :, slot_cols(c)], quarter_in.at[:, :, slot_cols(c)], sem_quarter.at[c]).wait()
+        pltpu.make_async_copy(quarter_in.at[:, :, slot_cols(c)], quarter_in.at[:, :, slot_cols(c)], sem_quarter.at[lax.rem(c, QUARTER_SEMS)]).wait()
         for d in range(1, n_chips):
             total = total + quarter_in[d - 1, :, slot_cols(c)].astype(F32)
         gather(c, total)
@@ -301,14 +303,14 @@
         out_buf[my_rows, quarter_cols(c, chip)] = total.astype(BF16)
         for d in sorted(range(1, n_tp), key=lambda d: -min(d, n_tp - d)):
             pltpu.make_async_remote_copy(src_ref=out_buf.at[my_rows, quarter_cols(c, chip)], dst_ref=out_buf.at[my_rows, quarter_cols(c, chip)],
-                                         send_sem=sem_sent.at[2], recv_sem=sem_gather.at[0],
+                                         send_sem=sem_sent.at[0], recv_sem=sem_gather.at[0],
                                          device_id={'tp': lax.rem(me + d, n_tp)}, device_id_type=pl.DeviceIdType.MESH).start()
 
     def send_direct(c):
         for d in sorted(range(1, n_tp), key=lambda d: -min(d, n_tp - d)):
             to = lax.rem(me + d, n_tp)
             src = part_buf.at[pl.ds(pl.multiple_of(lax.rem(to, 2) * half_rows, half_rows), half_rows), quarter_cols(c, to // 2)]
-            pltpu.make_async_remote_copy(src_ref=src, dst_ref=last_in.at[c - n_paired, d - 1], send_sem=sem_sent.at[3], recv_sem=sem_last.at[c - n_paired],
+            pltpu.make_async_remote_copy(src_ref=src, dst_ref=last_in.at[c - n_paired, d - 1], send_sem=sem_sent.at[0], recv_sem=sem_last.at[c - n_paired],
                                          device_id={'tp': to}, device_id_type=pl.DeviceIdType.MESH).start()
 
     def send_result_direct(c):
@@ -387,9 +389,9 @@
         sent = pltpu.make_async_copy(part_buf.at[other_rows, 0:n_paired * CHUNK], part_buf.at[other_rows, 0:n_paired * CHUNK], sem_sent.at[0])
         sent.wait()
         for d in range(1, n_chips):
-            pltpu.make_async_copy(quarter_in.at[d - 1, :, 0:n_paired * quarter], quarter_in.at[d - 1, :, 0:n_paired * quarter], sem_sent.at[1]).wait()
-        settle(sem_sent.at[2], (n_tp - 1) * rows // n_tp)
-        pltpu.make_async_copy(last_in, last_in, sem_sent.at[3]).wait()
+            pltpu.make_async_copy(quarter_in.at[d - 1, :, 0:n_paired * quarter], quarter_in.at[d - 1, :, 0:n_paired * quarter], sem_sent.at[0]).wait()
+        settle(sem_sent.at[0], (n_tp - 1) * rows // n_tp)
+        pltpu.make_async_copy(last_in, last_in, sem_sent.at[0]).wait()
 
 
 def write_kernel(a_ref, b_ref, c_ref, a_out, b_out, c_out, sem):
@@ -450,15 +452,15 @@
                 pltpu.VMEM((rows // 2, width), BF16),
                 pltpu.VMEM((n_chips - 1, rows // 2, width // n_chips), BF16),
                 pltpu.VMEM((N_DIRECT, n_tp - 1, rows // 2, CHUNK // n_chips), BF16),
-                pltpu.SemaphoreType.DMA((5,)),
+                pltpu.SemaphoreType.DMA((2,)),
                 pltpu.SemaphoreType.DMA((n_qkv // QKV_GROUP,)),
                 pltpu.SemaphoreType.DMA((A_SLOTS,)),
                 pltpu.SemaphoreType.DMA((A_SLOTS + B_SLOTS + 3,)),
-                pltpu.SemaphoreType.DMA((n_down - N_DIRECT,)),
-                pltpu.SemaphoreType.DMA((n_down - N_DIRECT,)),
+                pltpu.SemaphoreType.DMA((PAIR_SEMS,)),
+                pltpu.SemaphoreType.DMA((QUARTER_SEMS,)),
                 pltpu.SemaphoreType.DMA((1,)),
                 pltpu.SemaphoreType.DMA((N_DIRECT,)),
-                pltpu.SemaphoreType.DMA((4,)),
+                pltpu.SemaphoreType.DMA((1,)),
             ],
             compiler_params=pltpu.CompilerParams(vmem_limit_bytes=60 * 1024 * 1024, collective_id=0, has_side_effects=True),
         )(x, ga.reshape(1, width), ba.reshape(1, width), gm.reshape(1, width), bm.reshape(1, width), wq, wo, w_up, w_down, kt, vt, positions.reshape(1, rows))

time: 65.2 us -> 65 us (level)
  no operation moved by 1% of the time
where the time goes in v4:
time: 65 us
  Pallas kernels  64.3 us (99%)
    pallas_call x1, Pallas kernels, device_step(): pl.pallas_call(lambda *refs: layer_kernel(dims, *refs), name='layer', out...  62.6 us
    pallas_call x1, Pallas kernels, device_step(): pl.pallas_call(write_kernel, name='write', out_shape=(jax.ShapeDtypeStruc...  1.69 us

profile of v4, /device:TPU:81, one launch (start us, length us, event | category | flops | bytes accessed | tf_op | source)
XLA Modules:
  0.0 65.0 jit_solution(220557584184170671)
XLA Ops:
  0.6 62.6 %layer.1 = (bf16[64,8192]{1,0:T(8,128)(2,1)S(1)}, bf16[4096,128]{1,0:T(8,128)(2,1)S(1)}, bf16[4096,128]{1,0:T(8,128)(2,1)S(1)}) custom-call(bf16[64,8192]{1,0:T(8,128)(2,1)} %refs_0_.1, f32[1,8192]{1,0:T(1,128)} %bitcast.29, f32[1,8192]{1,0:T(1,128)} %bitcast.30, f32[1,8192]{1,0:T(1,128)} %bitcast.31, f32[1,8192]{1,0:T(1,128)} %bitcast.32, ...), custom_call_target="tpu_custom_call" | custom-call | tf_op jit(solution)/shard_map/layer/pallas_call | solution.py:430
  63.3 1.7 %write.1 = (bf16[64,8192]{1,0:T(8,128)(2,1)}, bf16[4096,128]{1,0:T(8,128)(2,1)}, bf16[4096,128]{1,0:T(8,128)(2,1)}) custom-call(bf16[64,8192]{1,0:T(8,128)(2,1)S(1)} %get-tuple-element.9.a_ref, bf16[4096,128]{1,0:T(8,128)(2,1)S(1)} %get-tuple-element.10.b_ref, bf16[4096,128]{1,0:T(8,128)(2,1)S(1)} %get-tuple-element.11.c_ref), custom_call_target="tpu_custom_call" | custom-call | tf_op jit(solution)/shard_map/write/pallas_call | solution.py:468

commit v5 on v4

--- a/solution.py
+++ b/solution.py
@@ -265,6 +265,12 @@
     act[:, ff:ff + CHUNK] = gelu_exact(pre[...]).astype(BF16)
 
     n_paired = n_down - N_DIRECT
+
+    far_first = sorted(range(1, n_tp), key=lambda d: -min(d // 2, n_chips - d // 2))
+
+    def peer(d):
+        return lax.rem(chip + d // 2, n_chips) * 2 + lax.rem(core + d % 2, 2)
+
     my_rows = pl.ds(pl.multiple_of(core * half_rows, half_rows), half_rows)
     other_rows = pl.ds(pl.multiple_of((1 - core) * half_rows, half_rows), half_rows)
 
@@ -301,14 +307,14 @@
 
     def gather(c, total):
         out_buf[my_rows, quarter_cols(c, chip)] = total.astype(BF16)
-        for d in sorted(range(1, n_tp), key=lambda d: -min(d, n_tp - d)):
+        for d in far_first:
             pltpu.make_async_remote_copy(src_ref=out_buf.at[my_rows, quarter_cols(c, chip)], dst_ref=out_buf.at[my_rows, quarter_cols(c, chip)],
                                          send_sem=sem_sent.at[0], recv_sem=sem_gather.at[0],
-                                         device_id={'tp': lax.rem(me + d, n_tp)}, device_id_type=pl.DeviceIdType.MESH).start()
+                                         device_id={'tp': peer(d)}, device_id_type=pl.DeviceIdType.MESH).start()
 
     def send_direct(c):
-        for d in sorted(range(1, n_tp), key=lambda d: -min(d, n_tp - d)):
-            to = lax.rem(me + d, n_tp)
+        for d in far_first:
+            to = peer(d)
             src = part_buf.at[pl.ds(pl.multiple_of(lax.rem(to, 2) * half_rows, half_rows), half_rows), quarter_cols(c, to // 2)]
             pltpu.make_async_remote_copy(src_ref=src, dst_ref=last_in.at[c - n_paired, d - 1], send_sem=sem_sent.at[0], recv_sem=sem_last.at[c - n_paired],
                                          device_id={'tp': to}, device_id_type=pl.DeviceIdType.MESH).start()

time: 65 us -> 65 us (level)
  no operation moved by 1% of the time
where the time goes in v5:
time: 65 us
  Pallas kernels  64.3 us (99%)
    pallas_call x1, Pallas kernels, device_step(): pl.pallas_call(lambda *refs: layer_kernel(dims, *refs), name='layer', out...  62.6 us
    pallas_call x1, Pallas kernels, device_step(): pl.pallas_call(write_kernel, name='write', out_shape=(jax.ShapeDtypeStruc...  1.69 us

profile of v5, /device:TPU:81, one launch (start us, length us, event | category | flops | bytes accessed | tf_op | source)
XLA Modules:
  0.0 65.0 jit_solution(944505761458186632)
XLA Ops:
  0.6 62.6 %layer.1 = (bf16[64,8192]{1,0:T(8,128)(2,1)S(1)}, bf16[4096,128]{1,0:T(8,128)(2,1)S(1)}, bf16[4096,128]{1,0:T(8,128)(2,1)S(1)}) custom-call(bf16[64,8192]{1,0:T(8,128)(2,1)} %refs_0_.1, f32[1,8192]{1,0:T(1,128)} %bitcast.29, f32[1,8192]{1,0:T(1,128)} %bitcast.30, f32[1,8192]{1,0:T(1,128)} %bitcast.31, f32[1,8192]{1,0:T(1,128)} %bitcast.32, ...), custom_call_target="tpu_custom_call" | custom-call | tf_op jit(solution)/shard_map/layer/pallas_call | solution.py:436
  63.3 1.7 %write.1 = (bf16[64,8192]{1,0:T(8,128)(2,1)}, bf16[4096,128]{1,0:T(8,128)(2,1)}, bf16[4096,128]{1,0:T(8,128)(2,1)}) custom-call(bf16[64,8192]{1,0:T(8,128)(2,1)S(1)} %get-tuple-element.9.a_ref, bf16[4096,128]{1,0:T(8,128)(2,1)S(1)} %get-tuple-element.10.b_ref, bf16[4096,128]{1,0:T(8,128)(2,1)S(1)} %get-tuple-element.11.c_ref), custom_call_target="tpu_custom_call" | custom-call | tf_op jit(solution)/shard_map/write/pallas_call | solution.py:474
